TPU v7x, 32 devices: a whole 2x2x4 slice. The times are simulated.
32 devices in a mesh: blk: 32 (over z, y, x, core).
Axes of the slice: x: 2, y: 2, z: 4, core: 2. Of those that a mesh axis runs over, the one named last changes fastest.
Arguments:
- queries: bfloat16 [2048, 4096], P('blk'), may hold values from -200 to 200
- keys: bfloat16 [2048, 2048], P('blk'), may hold values from -8 to 8
- values: bfloat16 [2048, 2048], P('blk'), may hold values from -6 to 6
- doc_start: int32 [2048], P('blk'), may hold values from 0 to 2047, as said below
Outputs:
- attended: bfloat16 [2048, 4096], P('blk')
Inputs may be any that keep to these rules, and one draw needn't show every extreme that they name: doc_start[i] is the first position of token i's document: nondecreasing, at most i, doc_start[doc_start[i]] = doc_start[i], and position 0 starts a document.
All inputs are finite; a program needn't handle non-finite values.
Results may differ from a plain program's by a relative error of at most 0.0034.
Values may be sent and summed in bfloat16 or wider, within the bound.
A program may use at most 64 MiB of HBM per device.

v0:
```python
import functools

import jax
import jax.numpy as jnp
from jax import lax
from jax.experimental import pallas as pl
from jax.experimental.pallas import tpu as pltpu
from jax.sharding import PartitionSpec as P

HD = 256
HOPS = 4
NEGATIVE = -1e30
MESH = pl.DeviceIdType.MESH


def kernel(
    n, q_hbm, k_hbm, v_hbm, doc_ref, out_ref,
    q_buf, kv, bias, q_sem, own_sem,
    y_send, y_recv, x_send, x_recv, o_send, o_recv, p_send, p_recv, pp_send, pp_recv,
):
    rows = q_hbm.shape[0]
    heads = k_hbm.shape[1] // HD
    groups = q_hbm.shape[1] // k_hbm.shape[1]
    window = HOPS * rows
    span = window + rows
    wide = groups * HD

    me = lax.axis_index("blk")
    core = lax.rem(me, 2)
    chip = me // 2
    odd = lax.rem(chip, 2)
    partner = me + 1 - 2 * core
    beside = me + 2 - 4 * odd
    has_far = me >= 4
    has_near = jnp.logical_or(odd == 1, has_far)
    sends_far = me + 4 < n
    far_to = lax.rem(me + 4, n)

    def slot(number):
        return pl.ds(pl.multiple_of(number * rows, rows), rows)

    def own_copy(h, which):
        src = (k_hbm, v_hbm)[which]
        columns = pl.ds(pl.multiple_of(h * HD, HD), HD)
        return pltpu.make_async_copy(
            src.at[:, columns], kv.at[h, which, slot(4 + core), :], own_sem.at[which, h]
        )

    def remote(h, source, target, send, recv, device):
        return pltpu.make_async_remote_copy(
            src_ref=kv.at[h, :, slot(source), :],
            dst_ref=kv.at[h, :, slot(target), :],
            send_sem=send.at[h],
            recv_sem=recv.at[h],
            device_id=(device,),
            device_id_type=MESH,
        )

    def far_copy(h):
        return remote(h, 4 + core, core, y_send, y_recv, far_to)

    def near_copy(h):
        return remote(h, core + 4 * (1 - odd), 2 + core, x_send, x_recv, beside)

    def share_own(h):
        return remote(h, 4, 4, o_send, o_recv, partner)

    def share_near(h):
        return remote(h, 2 + core, 2 + core, p_send, p_recv, partner)

    def near_shared(h):
        return remote(h, 3 - core, 3 - core, p_send, p_recv, partner)

    def share_far(h):
        return remote(h, 1, 1, pp_send, pp_recv, partner)

    def each_head(body):
        def step(h, carry):
            body(h)
            return carry

        lax.fori_loop(0, heads, step, 0)

    q_copy = pltpu.make_async_copy(q_hbm, q_buf, q_sem)

    def load(h):
        own_copy(h, 0).start()
        own_copy(h, 1).start()

    each_head(load)
    q_copy.start()

    barrier = pltpu.get_barrier_semaphore()

    def greet(device):
        pl.semaphore_signal(barrier, inc=1, device_id=(device,), device_id_type=MESH)

    greet(partner)
    greet(beside)

    @pl.when(sends_far)
    def _():
        greet(me + 4)

    @pl.when(has_far)
    def _():
        greet(me - 4)

    pl.semaphore_wait(barrier, 2 + jnp.where(sends_far, 1, 0) + jnp.where(has_far, 1, 0))

    def send(h):
        own_copy(h, 0).wait()
        own_copy(h, 1).wait()

        @pl.when(sends_far)
        def _():
            far_copy(h).start()

        @pl.when(odd == 0)
        def _():
            near_copy(h).start()

        @pl.when(core == 0)
        def _():
            share_own(h).start()

    each_head(send)

    @pl.when(me < 4)
    def _():
        def clear(h):
            kv[h, :, 0 : 2 * rows, :] = jnp.zeros((2, 2 * rows, HD), kv.dtype)

        each_head(clear)

    @pl.when(me < 2)
    def _():
        def clear(h):
            kv[h, :, 2 * rows : 4 * rows, :] = jnp.zeros((2, 2 * rows, HD), kv.dtype)

        each_head(clear)

    square_row = lax.broadcasted_iota(jnp.int32, (rows, rows), 0)
    square_col = lax.broadcasted_iota(jnp.int32, (rows, rows), 1)
    spread = jnp.broadcast_to(doc_ref[...], (rows, rows)).astype(jnp.float32)
    starts = jnp.sum(jnp.where(square_row == square_col, spread, 0.0), axis=1, keepdims=True)
    starts = starts.astype(jnp.int32)
    q_pos = me * rows + lax.broadcasted_iota(jnp.int32, (rows, span), 0)
    k_pos = (me - HOPS) * rows + lax.broadcasted_iota(jnp.int32, (rows, span), 1)
    allowed = (k_pos <= q_pos) & (q_pos - k_pos < window) & (k_pos >= starts)
    bias[...] = jnp.where(allowed, 0.0, NEGATIVE)
    q_copy.wait()

    def relay(h):
        @pl.when(has_far)
        def _():
            far_copy(h).wait_recv()

            @pl.when(odd == 1)
            def _():
                near_copy(h).start()

            @pl.when(core == 1)
            def _():
                share_far(h).start()

        @pl.when(has_near)
        def _():
            near_copy(h).wait_recv()
            share_near(h).start()

    def attend(h):
        @pl.when(has_near)
        def _():
            near_shared(h).wait_recv()

        @pl.when(jnp.logical_and(has_far, core == 0))
        def _():
            share_far(h).wait_recv()

        @pl.when(core == 1)
        def _():
            share_own(h).wait_recv()

        columns = pl.ds(pl.multiple_of(h * wide, wide), wide)
        query = q_buf[:, columns]
        query = jnp.concatenate(
            [query[:, g * HD : (g + 1) * HD] for g in range(groups)], axis=0
        )
        reach = pl.ds(pl.multiple_of(core * rows, rows), span)
        scores = lax.dot_general(
            query, kv[h, 0, reach, :], (((1,), (1,)), ((), ())),
            preferred_element_type=jnp.float32,
        ) * 0.0625
        hidden = jnp.concatenate([bias[...]] * groups, axis=0) < 0
        scores = jnp.where(hidden, NEGATIVE, scores)
        top = jnp.max(scores, axis=1, keepdims=True)
        expo = jnp.exp(scores - top)
        total = jnp.sum(expo, axis=1, keepdims=True)
        mixed = jnp.dot(
            expo.astype(jnp.bfloat16), kv[h, 1, reach, :],
            preferred_element_type=jnp.float32,
        )
        mixed = (mixed / total).astype(out_ref.dtype)
        out_ref[:, columns] = jnp.concatenate(
            [mixed[g * rows : (g + 1) * rows] for g in range(groups)], axis=1
        )

    def turn(h, carry):
        @pl.when(h < heads)
        def _():
            relay(h)

        @pl.when(h >= 1)
        def _():
            attend(h - 1)

        return carry

    lax.fori_loop(0, heads + 1, turn, 0)

    def drain(h):
        @pl.when(sends_far)
        def _():
            far_copy(h).wait_send()

        @pl.when(has_far)
        def _():
            @pl.when(core == 1)
            def _():
                share_far(h).wait_send()

        @pl.when(jnp.logical_or(odd == 0, has_far))
        def _():
            near_copy(h).wait_send()

        @pl.when(has_near)
        def _():
            share_near(h).wait_send()

        @pl.when(core == 0)
        def _():
            share_own(h).wait_send()

    each_head(drain)


def solution(mesh):
    n = mesh.shape["blk"]

    def per_device(queries, keys, values, doc_start):
        rows, columns = queries.shape
        heads = keys.shape[1] // HD
        span = (HOPS + 1) * rows
        remote_sems = [pltpu.SemaphoreType.DMA((heads,)) for _ in range(10)]
        return pl.pallas_call(
            functools.partial(kernel, n),
            out_shape=jax.ShapeDtypeStruct((rows, columns), jnp.bfloat16),
            in_specs=[pl.BlockSpec(memory_space=pl.ANY)] * 3
            + [pl.BlockSpec(memory_space=pltpu.VMEM)],
            out_specs=pl.BlockSpec(memory_space=pltpu.VMEM),
            scratch_shapes=[
                pltpu.VMEM((rows, columns), jnp.bfloat16),
                pltpu.VMEM((heads, 2, (HOPS + 2) * rows, HD), jnp.bfloat16),
                pltpu.VMEM((rows, span), jnp.float32),
                pltpu.SemaphoreType.DMA,
                pltpu.SemaphoreType.DMA((2, heads)),
            ]
            + remote_sems,
            compiler_params=pltpu.CompilerParams(collective_id=0, has_side_effects=True),
        )(queries, keys, values, doc_start.reshape(1, rows))

    return jax.shard_map(
        per_device,
        mesh=mesh,
        in_specs=(P("blk", None), P("blk", None), P("blk", None), P("blk")),
        out_specs=P("blk", None),
        check_vma=False,
    )
```

profile of v0, /device:TPU:9, one launch (start us, length us, event | category | flops | bytes accessed | tf_op | source)
XLA Modules:
  0.0 25.3 jit_solution(12258322488940876380)
XLA Ops:
  0.0 23.4 %shard_map.46 = bf16[64,4096]{1,0:T(8,128)(2,1)} custom-call(bf16[64,4096]{1,0:T(8,128)(2,1)} %q_hbm.1, bf16[64,2048]{1,0:T(8,128)(2,1)} %k_hbm.1, bf16[64,2048]{1,0:T(8,128)(2,1)} %v_hbm.1, s32[1,64]{1,0:T(1,128)} %bitcast.1), custom_call_target="tpu_custom_call" | custom-call | tf_op jit(solution)/shard_map/pallas_call | solution.py:256
  23.4 1.9 %copy.6 = bf16[64,4096]{1,0:T(8,128)(2,1)} copy(bf16[64,4096]{1,0:T(8,128)(2,1)} %shard_map.46) | data formatting | bytes 1048576
where the time goes:
time: 25.4 us; the launch traced here: 25.3 us
  Pallas kernels  23.4 us (92%)
  local copies, waits for them, and re-layouts  1.87 us (7%)
    pallas_call x1, Pallas kernels, per_device(): pl.pallas_call(functools.partial(kernel, n), out_shape=jax.ShapeDtypeStru...  23.4 us
    unnamed x1, local copies, waits for them, and re-layouts  1.87 us

commit v1 on v0

--- a/solution.py
+++ b/solution.py
@@ -10,12 +10,13 @@
 HD = 256
 HOPS = 4
 NEGATIVE = -1e30
+FORWARD_AT = 2
 MESH = pl.DeviceIdType.MESH
 
 
 def kernel(
     n, q_hbm, k_hbm, v_hbm, doc_ref, out_ref,
-    q_buf, kv, bias, q_sem, own_sem,
+    q_buf, kv, passing, passing_half, bias, q_sem, own_sem, half_sems, pass_send, pass_recv, onward_send, onward_recv,
     y_send, y_recv, x_send, x_recv, o_send, o_recv, p_send, p_recv, pp_send, pp_recv,
 ):
     rows = q_hbm.shape[0]
@@ -62,6 +63,64 @@
     def near_copy(h):
         return remote(h, core + 4 * (1 - odd), 2 + core, x_send, x_recv, beside)
 
+    last = heads - 2
+
+    def odd_order(i):
+        return jnp.where(i >= last, 2 * heads - 3 - i, i)
+
+    def order(i):
+        return jnp.where(odd == 1, odd_order(i), i)
+
+    def pass_copy():
+        return pltpu.make_async_remote_copy(
+            src_ref=kv.at[last, :, slot(4 + core), :],
+            dst_ref=passing,
+            send_sem=pass_send,
+            recv_sem=pass_recv,
+            device_id=(beside,),
+            device_id_type=MESH,
+        )
+
+    def half_pass():
+        return pltpu.make_async_remote_copy(
+            src_ref=kv.at[heads - 1, 1, slot(4 + core), :],
+            dst_ref=passing_half,
+            send_sem=half_sems.at[0],
+            recv_sem=half_sems.at[1],
+            device_id=(beside,),
+            device_id_type=MESH,
+        )
+
+    def half_onward():
+        return pltpu.make_async_remote_copy(
+            src_ref=passing_half,
+            dst_ref=kv.at[heads - 1, 1, slot(2 + core), :],
+            send_sem=half_sems.at[2],
+            recv_sem=half_sems.at[3],
+            device_id=(far_to,),
+            device_id_type=MESH,
+        )
+
+    def near_half():
+        return pltpu.make_async_remote_copy(
+            src_ref=kv.at[heads - 1, 0, slot(core + 4 * (1 - odd)), :],
+            dst_ref=kv.at[heads - 1, 0, slot(2 + core), :],
+            send_sem=half_sems.at[4],
+            recv_sem=half_sems.at[5],
+            device_id=(beside,),
+            device_id_type=MESH,
+        )
+
+    def onward_copy():
+        return pltpu.make_async_remote_copy(
+            src_ref=passing,
+            dst_ref=kv.at[last, :, slot(2 + core), :],
+            send_sem=onward_send,
+            recv_sem=onward_recv,
+            device_id=(far_to,),
+            device_id_type=MESH,
+        )
+
     def share_own(h):
         return remote(h, 4, 4, o_send, o_recv, partner)
 
@@ -81,6 +140,22 @@
 
         lax.fori_loop(0, heads, step, 0)
 
+    barrier = pltpu.get_barrier_semaphore()
+
+    def greet(device):
+        pl.semaphore_signal(barrier, inc=1, device_id=(device,), device_id_type=MESH)
+
+    @pl.when(sends_far)
+    def _():
+        greet(me + 4)
+
+    @pl.when(has_far)
+    def _():
+        greet(me - 4)
+
+    greet(beside)
+    greet(partner)
+
     q_copy = pltpu.make_async_copy(q_hbm, q_buf, q_sem)
 
     def load(h):
@@ -90,41 +165,40 @@
     each_head(load)
     q_copy.start()
 
-    barrier = pltpu.get_barrier_semaphore()
-
-    def greet(device):
-        pl.semaphore_signal(barrier, inc=1, device_id=(device,), device_id_type=MESH)
-
-    greet(partner)
-    greet(beside)
-
-    @pl.when(sends_far)
-    def _():
-        greet(me + 4)
-
-    @pl.when(has_far)
-    def _():
-        greet(me - 4)
-
     pl.semaphore_wait(barrier, 2 + jnp.where(sends_far, 1, 0) + jnp.where(has_far, 1, 0))
 
-    def send(h):
+    passes = jnp.logical_and(sends_far, odd == 1)
+    onward = jnp.logical_and(sends_far, odd == 0)
+    takes = jnp.logical_and(has_far, odd == 0)
+
+    def own_copy_wait(h):
         own_copy(h, 0).wait()
         own_copy(h, 1).wait()
 
+    each_head(own_copy_wait)
+
+    def send(i):
+        h, near_head = order(i), odd_order(i)
+
+
         @pl.when(sends_far)
         def _():
             far_copy(h).start()
 
         @pl.when(odd == 0)
         def _():
-            near_copy(h).start()
+            near_copy(near_head).start()
 
         @pl.when(core == 0)
         def _():
             share_own(h).start()
 
     each_head(send)
+
+    @pl.when(passes)
+    def _():
+        pass_copy().start()
+        half_pass().start()
 
     @pl.when(me < 4)
     def _():
@@ -156,17 +230,37 @@
         def _():
             far_copy(h).wait_recv()
 
-            @pl.when(odd == 1)
+            @pl.when(jnp.logical_and(odd == 1, h < last))
             def _():
                 near_copy(h).start()
 
+            @pl.when(jnp.logical_and(odd == 1, h > last))
+            def _():
+                near_half().start()
+
             @pl.when(core == 1)
             def _():
                 share_far(h).start()
 
         @pl.when(has_near)
         def _():
-            near_copy(h).wait_recv()
+            by_way = jnp.logical_and(takes, h == last)
+
+            @pl.when(by_way)
+            def _():
+                onward_copy().wait_recv()
+
+            by_halves = jnp.logical_and(takes, h > last)
+
+            @pl.when(by_halves)
+            def _():
+                near_half().wait_recv()
+                half_onward().wait_recv()
+
+            @pl.when(jnp.logical_not(jnp.logical_or(by_way, by_halves)))
+            def _():
+                near_copy(h).wait_recv()
+
             share_near(h).start()
 
     def attend(h):
@@ -207,13 +301,20 @@
         )
 
     def turn(h, carry):
+        @pl.when(jnp.logical_and(onward, h == FORWARD_AT))
+        def _():
+            pass_copy().wait_recv()
+            onward_copy().start()
+            half_pass().wait_recv()
+            half_onward().start()
+
         @pl.when(h < heads)
         def _():
-            relay(h)
+            relay(order(h))
 
         @pl.when(h >= 1)
         def _():
-            attend(h - 1)
+            attend(order(h - 1))
 
         return carry
 
@@ -230,7 +331,7 @@
             def _():
                 share_far(h).wait_send()
 
-        @pl.when(jnp.logical_or(odd == 0, has_far))
+        @pl.when(jnp.logical_or(odd == 0, jnp.logical_and(has_far, h < last)))
         def _():
             near_copy(h).wait_send()
 
@@ -243,6 +344,20 @@
             share_own(h).wait_send()
 
     each_head(drain)
+
+    @pl.when(passes)
+    def _():
+        pass_copy().wait_send()
+        half_pass().wait_send()
+
+    @pl.when(onward)
+    def _():
+        onward_copy().wait_send()
+        half_onward().wait_send()
+
+    @pl.when(jnp.logical_and(has_far, odd == 1))
+    def _():
+        near_half().wait_send()
 
 
 def solution(mesh):
@@ -255,17 +370,21 @@
         remote_sems = [pltpu.SemaphoreType.DMA((heads,)) for _ in range(10)]
         return pl.pallas_call(
             functools.partial(kernel, n),
-            out_shape=jax.ShapeDtypeStruct((rows, columns), jnp.bfloat16),
+            out_shape=pltpu.VMEM((rows, columns), jnp.bfloat16),
             in_specs=[pl.BlockSpec(memory_space=pl.ANY)] * 3
             + [pl.BlockSpec(memory_space=pltpu.VMEM)],
             out_specs=pl.BlockSpec(memory_space=pltpu.VMEM),
             scratch_shapes=[
                 pltpu.VMEM((rows, columns), jnp.bfloat16),
                 pltpu.VMEM((heads, 2, (HOPS + 2) * rows, HD), jnp.bfloat16),
+                pltpu.VMEM((2, rows, HD), jnp.bfloat16),
+                pltpu.VMEM((rows, HD), jnp.bfloat16),
                 pltpu.VMEM((rows, span), jnp.float32),
                 pltpu.SemaphoreType.DMA,
                 pltpu.SemaphoreType.DMA((2, heads)),
+                pltpu.SemaphoreType.DMA((6,)),
             ]
+            + [pltpu.SemaphoreType.DMA] * 4
             + remote_sems,
             compiler_params=pltpu.CompilerParams(collective_id=0, has_side_effects=True),
         )(queries, keys, values, doc_start.reshape(1, rows))

time: 25.4 us -> 22.4 us (0.88)
  Pallas kernels: 23.4 us -> 21.3 us
  local copies, waits for them, and re-layouts: 1.87 us -> 0.8 us
    pallas_call x1, Pallas kernels: 23.4 us -> 21.3 us  [per_device(): pl.pallas_call(functools.partial(kernel, n), out_shape=pltpu.VMEM((rows,...]
    unnamed x1, local copies, waits for them, and re-layouts: 1.87 us -> 0.8 us
where the time goes in v1:
time: 22.4 us; the launch traced here: 22.1 us
  Pallas kernels  21.3 us (95%)
  local copies, waits for them, and re-layouts  0.8 us (4%)
    pallas_call x1, Pallas kernels, per_device(): pl.pallas_call(functools.partial(kernel, n), out_shape=pltpu.VMEM((rows,...  21.3 us
    unnamed x1, local copies, waits for them, and re-layouts  0.8 us

profile of v1, /device:TPU:9, one launch (start us, length us, event | category | flops | bytes accessed | tf_op | source)
XLA Modules:
  0.0 22.1 jit_solution(6540592234638900652)
XLA Ops:
  0.0 21.3 %shard_map.46 = bf16[64,4096]{1,0:T(8,128)(2,1)S(1)} custom-call(bf16[64,4096]{1,0:T(8,128)(2,1)} %q_hbm.1, bf16[64,2048]{1,0:T(8,128)(2,1)} %k_hbm.1, bf16[64,2048]{1,0:T(8,128)(2,1)} %v_hbm.1, s32[1,64]{1,0:T(1,128)} %bitcast.1), custom_call_target="tpu_custom_call" | custom-call | tf_op jit(solution)/shard_map/pallas_call | solution.py:371
  21.3 0.8 %copy.6 = bf16[64,4096]{1,0:T(8,128)(2,1)} copy(bf16[64,4096]{1,0:T(8,128)(2,1)S(1)} %shard_map.46) | data formatting | bytes 1048576

commit v2 on v1

--- a/solution.py
+++ b/solution.py
@@ -295,7 +295,7 @@
             expo.astype(jnp.bfloat16), kv[h, 1, reach, :],
             preferred_element_type=jnp.float32,
         )
-        mixed = (mixed / total).astype(out_ref.dtype)
+        mixed = (mixed * (1.0 / total)).astype(out_ref.dtype)
         out_ref[:, columns] = jnp.concatenate(
             [mixed[g * rows : (g + 1) * rows] for g in range(groups)], axis=1
         )
@@ -312,13 +312,13 @@
         def _():
             relay(order(h))
 
-        @pl.when(h >= 1)
-        def _():
-            attend(order(h - 1))
+        @pl.when(h >= 2)
+        def _():
+            attend(order(h - 2))
 
         return carry
 
-    lax.fori_loop(0, heads + 1, turn, 0)
+    lax.fori_loop(0, heads + 2, turn, 0)
 
     def drain(h):
         @pl.when(sends_far)

time: 22.4 us -> 22.3 us (level)
  no operation moved by 1% of the time
where the time goes in v2:
time: 22.3 us; the launch traced here: 22.1 us
  Pallas kernels  21.3 us (96%)
  local copies, waits for them, and re-layouts  0.8 us (4%)
    pallas_call x1, Pallas kernels, per_device(): pl.pallas_call(functools.partial(kernel, n), out_shape=pltpu.VMEM((rows,...  21.3 us
    unnamed x1, local copies, waits for them, and re-layouts  0.8 us

profile of v2, /device:TPU:9, one launch (start us, length us, event | category | flops | bytes accessed | tf_op | source)
XLA Modules:
  0.0 22.1 jit_solution(4496484697581538012)
XLA Ops:
  0.0 21.3 %shard_map.46 = bf16[64,4096]{1,0:T(8,128)(2,1)S(1)} custom-call(bf16[64,4096]{1,0:T(8,128)(2,1)} %q_hbm.1, bf16[64,2048]{1,0:T(8,128)(2,1)} %k_hbm.1, bf16[64,2048]{1,0:T(8,128)(2,1)} %v_hbm.1, s32[1,64]{1,0:T(1,128)} %bitcast.1), custom_call_target="tpu_custom_call" | custom-call | tf_op jit(solution)/shard_map/pallas_call | solution.py:371
  21.3 0.8 %copy.6 = bf16[64,4096]{1,0:T(8,128)(2,1)} copy(bf16[64,4096]{1,0:T(8,128)(2,1)S(1)} %shard_map.46) | data formatting | bytes 1048576
